TPU v7x, 32 devices: a whole 2x2x4 slice. The times are simulated.
32 devices in a mesh: dp: 16 (over z, y, core), seq: 2 (over x).
Axes of the slice: x: 2, y: 2, z: 4, core: 2. Of those that a mesh axis runs over, the one named last changes fastest.
Arguments:
- fields: bfloat16 [16, 1024, 276], P('dp', 'seq'), may hold values from -6 to 6
- targets: float32 [16, 1024, 276], P('dp', 'seq'), may hold values from -6 to 6
- counts: int32 [16, 5], P('dp'), may hold values from 5 to 13
- lead_step: int32 [16], P('dp'), may hold values from 0 to 7
- step_count: int32 [], replicated, may hold values from 2 to 20
- attention_mats: float32 [4, 384, 384], P(None, 'dp')
- attention_mom: float32 [4, 384, 384], P(None, 'dp'), may hold values from -3.33786e-06 to 3.33786e-06
- feedforward_mats: float32 [2, 384, 1536], P(None, 'dp'), may hold values from -0.3125 to 0.3125
- feedforward_mom: float32 [2, 384, 1536], P(None, 'dp'), may hold values from -3.33786e-06 to 3.33786e-06
- modulation_mat: float32 [384, 2304], P('dp'), may hold values from -0.3125 to 0.3125
- modulation_first: float32 [384, 2304], P('dp'), may hold values from -3.5762787e-07 to 3.5762787e-07
- modulation_second: float32 [384, 2304], P('dp'), may hold values from 1.65e-14 to 6.6e-14
- pooling_mats: float32 [2, 384, 384], P(None, 'dp'), may hold values from -0.625 to 0.625
- pooling_first: float32 [2, 384, 384], P(None, 'dp'), may hold values from -3.5762787e-07 to 3.5762787e-07
- pooling_second: float32 [2, 384, 384], P(None, 'dp'), may hold values from 1.65e-14 to 6.6e-14
- lookup_table: float32 [641, 384], P(None, 'dp')
- table_first: float32 [641, 384], P(None, 'dp'), may hold values from -3.5762787e-07 to 3.5762787e-07
- table_second: float32 [641, 384], P(None, 'dp'), may hold values from 1.65e-14 to 6.6e-14
Outputs:
- loss: float32 [], replicated
- grad_norm: float32 [], replicated
- attention_new: float32 [4, 384, 384], P(None, 'dp')
- attention_fresh: float32 [4, 384, 384], P(None, 'dp')
- feedforward_new: float32 [2, 384, 1536], P(None, 'dp')
- feedforward_fresh: float32 [2, 384, 1536], P(None, 'dp')
- modulation_new: float32 [384, 2304], P('dp')
- modulation_first_new: float32 [384, 2304], P('dp')
- modulation_second_new: float32 [384, 2304], P('dp')
- pooling_new: float32 [2, 384, 384], P(None, 'dp')
- pooling_first_new: float32 [2, 384, 384], P(None, 'dp')
- pooling_second_new: float32 [2, 384, 384], P(None, 'dp')
- table_new: float32 [641, 384], P(None, 'dp')
- table_first_new: float32 [641, 384], P(None, 'dp')
- table_second_new: float32 [641, 384], P(None, 'dp')
Inputs may be any that keep to these rules, and one draw needn't show every extreme that they name: Levels 0 to counts - 1 of each atmospheric variable are present, the others missing.
All inputs are finite; a program needn't handle non-finite values.
Results may differ from a plain program's by a relative error of at most 0.0097.
Values may be sent and summed in bfloat16 or wider, within the bound.
A program may use at most 128 MiB of HBM per device.

v0:
```python
import math

import jax
import jax.numpy as jnp
from jax import lax
from jax.sharding import PartitionSpec as P

D = 384
HEADS = 6
SURF = 4
LEVELS = 13
PATCH_PIX = 4
NLEAD = 8
PCOLS = 128
VARS = 69


norm_eps = 1e-06
clip_limit = 0.001
muon_mu = 0.95
muon_rate = 0.6
muon_decay = 0.01
adam_rate = 0.05
adam_one = 0.9
adam_two = 0.95
adam_eps = 1e-08
adam_decay = 0.1
ns_a = 3.4445
ns_b = -4.775
ns_c = 2.0315
mask_fill = -1000000000.0
highest = lax.Precision.HIGHEST


def high_dot(a, b):
    return jnp.dot(a, b, precision=highest, preferred_element_type=jnp.float32)


def plain_dot(a, b):
    return jnp.dot(a, b, preferred_element_type=jnp.float32)


def contract_last(a, b):
    return lax.dot_general(a, b, (((1,), (1,)), ((), ())), preferred_element_type=jnp.float32)


def contract_first(a, b):
    return lax.dot_general(a, b, (((0,), (0,)), ((), ())), preferred_element_type=jnp.float32)


def layer_norm(values):
    average = jnp.mean(values, axis=-1, keepdims=True)
    centered = values - average
    return centered * lax.rsqrt(jnp.mean(centered * centered, axis=-1, keepdims=True) + norm_eps)


def offsets():
    width_in = VARS * PATCH_PIX
    lead_at = width_in + VARS
    query_at = lead_at + NLEAD
    bias_at = query_at + HEADS
    head_at = bias_at + 6
    return (width_in, lead_at, query_at, bias_at, head_at)


def presence(count_row):
    levels = jnp.arange(LEVELS, dtype=jnp.int32)
    table_grid = (levels[None, :] < count_row[:, None]).astype(jnp.float32).reshape(-1)
    return jnp.concatenate([jnp.ones((SURF,), jnp.float32), table_grid])


def lat_weight(first_row, count, grid_rows):
    patch = first_row + jnp.arange(count, dtype=jnp.int32)
    pix_row = 2 * (patch // PCOLS)[:, None] + (jnp.arange(PATCH_PIX, dtype=jnp.int32) // 2)[None, :]
    angle = ((pix_row.astype(jnp.float32) + 0.5) / grid_rows - 0.5) * math.pi
    return jnp.cos(angle)


def aggregate(lookup, value_w, out_w, pix_rows, present):
    width_in, lead_at, query_at, bias_at, head_at = offsets()
    count = pix_rows.shape[0]
    head_dim = D // HEADS
    embedding = lookup[:width_in]
    var_bias = lookup[width_in:lead_at]
    pool_query = lookup[query_at:bias_at]
    select = (
        (jnp.arange(width_in, dtype=jnp.int32) // PATCH_PIX)[:, None]
        == jnp.arange(VARS, dtype=jnp.int32)[None, :]
    ).astype(jnp.float32)
    key_embed = contract_last_high(embedding, pool_query) / math.sqrt(D)
    key_block = (key_embed[:, :, None] * select[:, None, :]).reshape(width_in, HEADS * VARS)
    key_bias = contract_last_high(pool_query, var_bias) / math.sqrt(D)
    val_embed = high_dot(embedding, value_w).reshape(width_in, HEADS, head_dim)
    val_bias = high_dot(var_bias, value_w).reshape(VARS, HEADS, head_dim)
    scores = high_dot(pix_rows, key_block).reshape(count, HEADS, VARS) + key_bias[None]
    scores = jnp.where(present[None, None, :] > 0.5, scores, mask_fill)
    mixing = jax.nn.softmax(scores, axis=-1)
    repeated = high_dot(mixing.reshape(count * HEADS, VARS), select.T).reshape(
        count, HEADS, width_in
    )
    spread = repeated * pix_rows[:, None, :]
    pooled = jnp.einsum("nhk,khc->nhc", spread, val_embed, precision=highest)
    pooled = pooled + jnp.einsum("nhv,vhc->nhc", mixing, val_bias, precision=highest)
    return high_dot(pooled.reshape(count, D), out_w)


def contract_last_high(a, b):
    return lax.dot_general(
        a, b, (((1,), (1,)), ((), ())), precision=highest, preferred_element_type=jnp.float32
    )


def modulation(lookup, mod_mat, lead_index):
    width_in, lead_at, query_at, bias_at, head_at = offsets()
    lead_row = lax.dynamic_index_in_dim(lookup, lead_at + lead_index, 0, keepdims=False)
    condition = jax.nn.silu(lead_row)
    return high_dot(condition[None, :], mod_mat).reshape(6, D) + lookup[bias_at:head_at]


def entry_fn(stream, modul):
    return layer_norm(stream) * (1.0 + modul[1]) + modul[0]


def middle_fn(stream, modul, branch):
    stream_mid = stream + modul[2] * branch
    return (stream_mid, layer_norm(stream_mid) * (1.0 + modul[4]) + modul[3])


def closing_fn(stream, modul, lowered):
    return layer_norm(stream + modul[5] * lowered)


def orthogonalize(matrix):
    current = matrix / (jnp.sqrt(jnp.sum(matrix * matrix)) + 1e-07)
    for sweep in range(5):
        gram = high_dot(current, current.T)
        polynomial = ns_b * gram + ns_c * high_dot(gram, gram)
        current = ns_a * current + high_dot(polynomial, current)
    return current


def adamw(weight, first, second, gradient, step_count):
    first_new = adam_one * first + (1.0 - adam_one) * gradient
    second_new = adam_two * second + (1.0 - adam_two) * gradient * gradient
    steps_done = step_count.astype(jnp.float32)
    first_hat = first_new / (1.0 - adam_one**steps_done)
    second_hat = second_new / (1.0 - adam_two**steps_done)
    weight_new = weight - adam_rate * (
        first_hat / (jnp.sqrt(second_hat) + adam_eps) + adam_decay * weight
    )
    return (weight_new, first_new, second_new)


def body(
    fields,
    targets,
    counts,
    lead_step,
    step_count,
    attention_mats,
    attention_mom,
    feedforward_mats,
    feedforward_mom,
    modulation_mat,
    modulation_first,
    modulation_second,
    pooling_mats,
    pooling_first,
    pooling_second,
    lookup_table,
    table_first,
    table_second,
):
    seq_count = lax.axis_size("seq")
    data_count = lax.axis_size("dp")
    rows = fields.shape[1]
    length = rows * seq_count
    head_dim = D // HEADS
    scale = 1.0 / math.sqrt(head_dim)
    width_in, lead_at, query_at, bias_at, head_at = offsets()
    gathered = (
        lax.all_gather(attention_mats.astype(jnp.bfloat16), "dp", axis=1, tiled=True),
        lax.all_gather(feedforward_mats.astype(jnp.bfloat16), "dp", axis=1, tiled=True),
        lax.all_gather(modulation_mat.astype(jnp.bfloat16), "dp", axis=0, tiled=True),
        lax.all_gather(pooling_mats.astype(jnp.bfloat16), "dp", axis=1, tiled=True),
        lax.all_gather(lookup_table.astype(jnp.bfloat16), "dp", axis=1, tiled=True),
    )
    attention_b, feed_b, mod_b, pool_b, lookup_b = gathered
    present = presence(counts[0])
    first_row = lax.axis_index("seq") * rows
    lat = lat_weight(first_row, rows, 2 * length // PCOLS)
    weight = (lat[:, None, :] * present[None, :, None]).reshape(rows, width_in)
    weight_total = lax.psum(jnp.sum(weight), ("dp", "seq"))
    pix_rows = fields[0].astype(jnp.float32)

    def prelude(lookup_f, mod_f, pool_f):
        return (
            aggregate(lookup_f, pool_f[0], pool_f[1], pix_rows, present),
            modulation(lookup_f, mod_f, lead_step[0]),
        )

    (stream_in, modul), prelude_back = jax.vjp(
        prelude, lookup_b.astype(jnp.float32), mod_b.astype(jnp.float32), pool_b.astype(jnp.float32)
    )
    entry, entry_back = jax.vjp(entry_fn, stream_in, modul)
    entry_b = entry.astype(jnp.bfloat16)
    joined = jnp.concatenate([attention_b[0], attention_b[1], attention_b[2]], axis=1)
    triple = plain_dot(entry_b, joined)
    queries = triple[:, :D].astype(jnp.bfloat16).reshape(rows, HEADS, head_dim)
    keys = triple[:, D : 2 * D].astype(jnp.bfloat16)
    values = triple[:, 2 * D :].astype(jnp.bfloat16)
    keys_all, values_all = (
        lax.all_gather(keys, "seq", axis=0, tiled=True),
        lax.all_gather(values, "seq", axis=0, tiled=True),
    )
    block = math.gcd(512, length)
    pairs = (
        keys_all.reshape(length // block, block, HEADS, head_dim),
        values_all.reshape(length // block, block, HEADS, head_dim),
    )

    def block_scores(query_part, key_block):
        return (
            jnp.einsum("qhc,khc->hqk", query_part, key_block, preferred_element_type=jnp.float32)
            * scale
        )

    def totals_step(carry, key_block):
        running, total = carry
        scores = block_scores(queries, key_block)
        top = jnp.maximum(running, jnp.max(scores, axis=-1))
        total = total * jnp.exp(running - top) + jnp.sum(jnp.exp(scores - top[:, :, None]), axis=-1)
        return ((top, total), None)

    start = (jnp.full((HEADS, rows), -jnp.inf, jnp.float32), jnp.zeros((HEADS, rows), jnp.float32))
    (top, total), unused = lax.scan(totals_step, start, pairs[0])
    log_total = top + jnp.log(total)

    def probs_of(key_block):
        return jnp.exp(block_scores(queries, key_block) - log_total[:, :, None])

    def output_step(carry, pair):
        probs_b = probs_of(pair[0]).astype(jnp.bfloat16)
        return (
            carry
            + jnp.einsum("hqk,khc->qhc", probs_b, pair[1], preferred_element_type=jnp.float32),
            None,
        )

    attended, unused = lax.scan(output_step, jnp.zeros((rows, HEADS, head_dim), jnp.float32), pairs)
    attended_b = attended.reshape(rows, D).astype(jnp.bfloat16)
    branch = plain_dot(attended_b, attention_b[3])
    (stream_mid, inner), middle_back = jax.vjp(middle_fn, stream_in, modul, branch)
    inner_b = inner.astype(jnp.bfloat16)
    upper = plain_dot(inner_b, feed_b[0])
    hidden, gelu_back = jax.vjp(jax.nn.gelu, upper)
    hidden_b = hidden.astype(jnp.bfloat16)
    lowered = contract_last(hidden_b, feed_b[1])
    final, closing_back = jax.vjp(closing_fn, stream_mid, modul, lowered)
    final_b = final.astype(jnp.bfloat16)
    head_b = lookup_b[head_at:]
    pred = contract_last(final_b, head_b)
    miss = pred - targets[0]
    loss_part = jnp.sum(weight * miss * miss)
    dpred_b = (2.0 * weight * miss / weight_total).astype(jnp.bfloat16)
    dfinal = plain_dot(dpred_b, head_b)
    dhead = contract_first(dpred_b, final_b)
    dstream_c, dmodul_c, dlowered = closing_back(dfinal)
    dlowered_b = dlowered.astype(jnp.bfloat16)
    dhidden = plain_dot(dlowered_b, feed_b[1])
    ddown = contract_first(dlowered_b, hidden_b)
    dupper_b = gelu_back(dhidden)[0].astype(jnp.bfloat16)
    dinner = contract_last(dupper_b, feed_b[0])
    dup = contract_first(inner_b, dupper_b)
    dstream_m, dmodul_m, dbranch = middle_back((dstream_c, dinner))
    dbranch_b = dbranch.astype(jnp.bfloat16)
    dattended_b = (
        contract_last(dbranch_b, attention_b[3]).astype(jnp.bfloat16).reshape(rows, HEADS, head_dim)
    )
    dout_w = contract_first(attended_b, dbranch_b)

    def block_dprobs(grad_part, value_block):
        return jnp.einsum(
            "qhc,khc->hqk", grad_part, value_block, preferred_element_type=jnp.float32
        )

    def delta_step(carry, pair):
        return (
            carry + jnp.sum(probs_of(pair[0]) * block_dprobs(dattended_b, pair[1]), axis=-1),
            None,
        )

    delta, unused = lax.scan(delta_step, jnp.zeros((HEADS, rows), jnp.float32), pairs)

    def grad_step(carry, pair):
        key_block, value_block = pair
        probs = probs_of(key_block)
        dscores_b = (probs * (block_dprobs(dattended_b, value_block) - delta[:, :, None])).astype(
            jnp.bfloat16
        )
        dqueries = (
            carry
            + jnp.einsum("hqk,khc->qhc", dscores_b, key_block, preferred_element_type=jnp.float32)
            * scale
        )
        dkey_block = (
            jnp.einsum("hqk,qhc->khc", dscores_b, queries, preferred_element_type=jnp.float32)
            * scale
        )
        dvalue_block = jnp.einsum(
            "hqk,qhc->khc",
            probs.astype(jnp.bfloat16),
            dattended_b,
            preferred_element_type=jnp.float32,
        )
        return (dqueries, (dkey_block, dvalue_block))

    dqueries, (dkey_stack, dvalue_stack) = lax.scan(
        grad_step, jnp.zeros((rows, HEADS, head_dim), jnp.float32), pairs
    )
    dkeys_own, dvalues_own = (
        lax.psum_scatter(
            dkey_stack.reshape(length, D).astype(jnp.bfloat16),
            "seq",
            scatter_dimension=0,
            tiled=True,
        ).astype(jnp.float32),
        lax.psum_scatter(
            dvalue_stack.reshape(length, D).astype(jnp.bfloat16),
            "seq",
            scatter_dimension=0,
            tiled=True,
        ).astype(jnp.float32),
    )
    dtriple_b = jnp.concatenate([dqueries.reshape(rows, D), dkeys_own, dvalues_own], axis=1).astype(
        jnp.bfloat16
    )
    dentry = contract_last(dtriple_b, joined)
    djoined = contract_first(entry_b, dtriple_b)
    dstream_e, dmodul_e = entry_back(dentry)
    dlookup, dmod, dpool = prelude_back((dstream_m + dstream_e, dmodul_c + dmodul_m + dmodul_e))
    dlookup = dlookup + jnp.pad(dhead, ((head_at, 0), (0, 0)))
    grads = (
        jnp.stack([djoined[:, :D], djoined[:, D : 2 * D], djoined[:, 2 * D :], dout_w]),
        jnp.stack([dup, ddown]),
        dmod,
        dpool,
        dlookup,
    )
    dims = (1, 1, 0, 1, 1)
    totals = lax.psum((grads[0], grads[1], grads[2], grads[3], grads[4]), ("dp", "seq"))
    place = lax.axis_index("dp")
    shares = tuple(
        (
            lax.dynamic_slice_in_dim(
                whole,
                place * (whole.shape[axis] // data_count),
                whole.shape[axis] // data_count,
                axis,
            )
            for whole, axis in zip(totals, dims)
        )
    )
    square_part = jnp.float32(0.0)
    for share in shares:
        square_part = square_part + jnp.sum(share * share)
    loss_total = lax.psum(loss_part, ("dp", "seq"))
    square_total = lax.psum(square_part, "dp")
    loss = loss_total / weight_total
    grad_norm = jnp.sqrt(square_total)
    factor = clip_limit / jnp.maximum(grad_norm, clip_limit)
    clipped = [share * factor for share in shares]
    attention_fresh = muon_mu * attention_mom + clipped[0]
    feedforward_fresh = muon_mu * feedforward_mom + clipped[1]
    whole_attention, whole_feed = (
        lax.all_gather(attention_fresh, "dp", axis=1, tiled=True),
        lax.all_gather(feedforward_fresh, "dp", axis=1, tiled=True),
    )
    rows_own = attention_mom.shape[1]
    row_start = lax.axis_index("dp") * rows_own
    attention_orth = lax.dynamic_slice_in_dim(
        jax.vmap(orthogonalize)(whole_attention), row_start, rows_own, 1
    )
    feed_orth = lax.dynamic_slice_in_dim(
        jax.vmap(orthogonalize)(whole_feed), row_start, rows_own, 1
    )
    attention_new = attention_mats * (1.0 - muon_rate * muon_decay) - muon_rate * attention_orth
    feedforward_new = feedforward_mats * (1.0 - muon_rate * muon_decay) - muon_rate * feed_orth
    modulation_new, modulation_first_new, modulation_second_new = adamw(
        modulation_mat, modulation_first, modulation_second, clipped[2], step_count
    )
    pooling_new, pooling_first_new, pooling_second_new = adamw(
        pooling_mats, pooling_first, pooling_second, clipped[3], step_count
    )
    table_new, table_first_new, table_second_new = adamw(
        lookup_table, table_first, table_second, clipped[4], step_count
    )
    return (
        loss,
        grad_norm,
        attention_new,
        attention_fresh,
        feedforward_new,
        feedforward_fresh,
        modulation_new,
        modulation_first_new,
        modulation_second_new,
        pooling_new,
        pooling_first_new,
        pooling_second_new,
        table_new,
        table_first_new,
        table_second_new,
    )


def solution(mesh):
    placed = (
        P("dp", "seq", None),
        P("dp", "seq", None),
        P("dp", None),
        P("dp"),
        P(),
        P(None, "dp", None),
        P(None, "dp", None),
        P(None, "dp", None),
        P(None, "dp", None),
        P("dp", None),
        P("dp", None),
        P("dp", None),
        P(None, "dp", None),
        P(None, "dp", None),
        P(None, "dp", None),
        P(None, "dp"),
        P(None, "dp"),
        P(None, "dp"),
    )
    return jax.shard_map(
        body,
        mesh=mesh,
        in_specs=placed,
        out_specs=(
            P(),
            P(),
            P(None, "dp", None),
            P(None, "dp", None),
            P(None, "dp", None),
            P(None, "dp", None),
            P("dp", None),
            P("dp", None),
            P("dp", None),
            P(None, "dp", None),
            P(None, "dp", None),
            P(None, "dp", None),
            P(None, "dp"),
            P(None, "dp"),
            P(None, "dp"),
        ),
        check_vma=False,
    )
```

profile of v0, /device:TPU:0, one launch (start us, length us, event | category | flops | bytes accessed | tf_op | source)
XLA Modules:
  0.0 846.2 jit_solution(8768612907609724839)
XLA Ops:
  13.2 24.9 %all_gather.27 = bf16[641,384]{0,1:T(8,128)(2,1)S(1)} all-gather(bf16[641,24]{0,1:T(8,128)(2,1)S(1)} %convert_element_type.118), channel_id=1, replica_groups=mesh['dp'=16,'seq'=2] {'dp'}, dimensions={1}, use_global_device_ids=true | all-gather | bytes 523056 | tf_op jit(solution)/shard_map/all_gather | solution.py:186
  38.6 19.4 %all_gather.28 = bf16[2,384,384]{2,1,0:T(8,128)(2,1)S(1)} all-gather(bf16[2,24,384]{2,1,0:T(8,128)(2,1)S(1)} %convert_element_type.119), channel_id=1, replica_groups=mesh['dp'=16,'seq'=2] {'dp'}, dimensions={1}, use_global_device_ids=true | all-gather | bytes 626688 | tf_op jit(solution)/shard_map/all_gather | solution.py:185
  86.7 9.2 %all-gather.6.cloned.1.call-done = bf16[384,2304]{1,0:T(8,128)(2,1)} async-done(((bf16[24,2304]{1,0:T(8,128)(2,1)}), bf16[384,2304]{1,0:T(8,128)(2,1)}) %all-gather.6.cloned.1.call-update) | async-done | bytes 1769488 | tf_op jit(solution)/shard_map/all_gather | solution.py:184
  108.7 11.9 %all_gather.32 = bf16[1024,384]{1,0:T(8,128)(2,1)S(1)} all-gather(bf16[512,384]{1,0:T(8,128)(2,1)S(1)} %get-tuple-element.554), channel_id=1, replica_groups=mesh['dp'=16,'seq'=2] {'seq'}, dimensions={0}, use_global_device_ids=true | all-gather | bytes 1179648 | tf_op jit(solution)/shard_map/all_gather | solution.py:213
  123.6 11.2 %all_gather.31 = bf16[1024,384]{1,0:T(8,128)(2,1)S(1)} all-gather(bf16[512,384]{1,0:T(8,128)(2,1)} %get-tuple-element.555), channel_id=1, replica_groups=mesh['dp'=16,'seq'=2] {'seq'}, dimensions={0}, use_global_device_ids=true | all-gather | bytes 1179648 | tf_op jit(solution)/shard_map/all_gather | solution.py:214
  144.8 6.4 while.51
  164.0 38.5 %all-reduce.14 = (f32[]{:T(128)}, f32[]{:T(128)}) all-reduce(f32[]{:T(128)} %get-tuple-element.568, f32[]{:T(128)} %multiply_reduce_fusion.15), channel_id=1, replica_groups=mesh['dp'=16,'seq'=2] {'dp','seq'}, use_global_device_ids=true, to_apply=%region_15.16 | all-reduce | flops 2 | bytes 16 | tf_op jit(solution)/shard_map/psum | solution.py:367
  223.1 5.8 while.52
  228.9 14.7 %while.53 = (s32[]{:T(128)}, f32[512,6,64]{0,2,1:T(8,128)}, bf16[2,512,6,64]{1,3,2,0:T(8,128)(2,1)}, bf16[2,512,6,64]{1,3,2,0:T(8,128)(2,1)}, bf16[2,512,6,64]{1...) while((s32[]{:T(128)}, f32[512,6,64]{0,2,1:T(8,128)}, ...), condition=%wide.region_26.27_spmd.clone, body=%wide.region_25.26_spmd.clone.sunk | while | flops 1020002304 | bytes 56279388 | solution.py:318
  265.3 19.6 %reduce-scatter.3.cloned.1.call-done = bf16[512,384]{0,1:T(8,128)(2,1)} async-done(((bf16[1024,384]{0,1:T(8,128)(2,1)}), bf16[512,384]{0,1:T(8,128)(2,1)}) %reduce-scatter.3.cloned.1.call-update) | async-done | bytes 393232 | tf_op jit(solution)/shard_map/reduce_scatter | solution.py:322
  336.8 236.7 %all-reduce.18.cloned.1.call-done = (f32[4,384,384]{2,1,0:T(8,128)}, f32[2,384,1536]{2,1,0:T(8,128)}, f32[384,2304]{1,0:T(8,128)}, f32[2,384,384]{2,1,0:T(8,128)}, f32[641,384]{0,1:T(8,128)}) async-done(((f32[4,384,384]{2,1,0:T(8,128)}, f32[2,384,1536]{2,1,0:T(8,128)}, f32[384,2304]{1,0:T(8,128)}, f32[2,384,384]{2,1,0:T(8,128)}, f32[641,384]{0,1:T(8,128)}), (f32[4,384,384]{2,1,0:T(8,128)}, ...) | async-done | bytes 12781072 | tf_op jit(solution)/shard_map/psum | solution.py:351
  584.6 31.7 %psum.63 = f32[]{:T(128)} all-reduce(f32[]{:T(128)S(6)} %add.429), channel_id=1, replica_groups=mesh['dp'=16,'seq'=2] {'dp'}, use_global_device_ids=true, to_apply=%region_50.51 | all-reduce | flops 1 | bytes 8 | tf_op jit(solution)/shard_map/psum | solution.py:368
  627.7 31.2 %all-gather.12.cloned.1.call-done = f32[4,384,384]{2,1,0:T(8,128)} async-done(((f32[4,24,384]{2,1,0:T(8,128)}), f32[4,384,384]{2,1,0:T(8,128)}) %all-gather.12.cloned.1.call-update) | async-done | bytes 2359312 | tf_op jit(solution)/shard_map/all_gather | solution.py:376
  730.9 5.3 fusion.70
  740.7 7.9 fusion.124
  751.2 8.8 %multiply_add_fusion.3 = f32[2,384,1536]{2,1,0:T(8,128)S(1)} fusion(f32[2,384,384]{2,1,0:T(8,128)S(1)} %fusion.105, f32[2,384,1536]{2,1,0:T(8,128)S(1)} %copy-done.25, f32[2]{0:T(128)S(1)} %sqrt_add_fusion), kind=kOutput, calls=%fused_computation.62 | convolution fusion | flops 5440536576 | bytes 10616840 | tf_op jit(solution)/shard_map/vmap()/dot_general | solution.py:36
  760.0 8.1 fusion.247
  770.7 8.6 %multiply_add_fusion.2 = f32[2,384,1536]{2,1,0:T(8,128)S(1)} fusion(f32[2,384,1536]{2,1,0:T(8,128)S(1)} %multiply_add_fusion.3, f32[2,384,384]{2,1,0:T(8,128)S(1)} %fusion.104), kind=kOutput, calls=%fused_computation.61 | convolution fusion | flops 5438177280 | bytes 10616832 | tf_op jit(solution)/shard_map/vmap()/dot_general | solution.py:36
  779.3 7.9 fusion.248
  789.7 8.4 multiply_add_fusion.1
  798.2 8.1 fusion.249
  808.8 8.6 %multiply_add_fusion = f32[2,384,1536]{2,1,0:T(8,128)S(1)} fusion(f32[2,384,1536]{2,1,0:T(8,128)S(1)} %multiply_add_fusion.1, f32[2,384,384]{2,1,0:T(8,128)S(1)} %fusion.102), kind=kOutput, calls=%fused_computation.59 | convolution fusion | flops 5438177280 | bytes 10616832 | tf_op jit(solution)/shard_map/vmap()/dot_general | solution.py:36
  817.4 7.9 fusion.250
  827.9 8.2 fusion.251
  (491 shorter events, 302.6 us)
Async XLA Ops:
  7.2 31.4 %copy-start.80 = (f32[2,24,384]{2,1,0:T(8,128)S(1)}, f32[2,24,384]{2,1,0:T(8,128)}, u32[]{:S(2)}) copy-start(f32[2,24,384]{2,1,0:T(8,128)} %param.38) | copy-start | bytes 221188
  7.2 77.5 %all-gather.8.cloned.1.call-start = ((), (), s32[]{:S(2)}) async-start(), calls=%async_computation.3 | async-start | bytes 1253376 | tf_op jit(solution)/shard_map/all_gather | solution.py:182
  8.8 87.1 %all-gather.6.cloned.1.call-start = ((), (), s32[]{:S(2)}) async-start(), calls=%async_computation.2 | async-start | bytes 1880064 | tf_op jit(solution)/shard_map/all_gather | solution.py:184
  10.5 145.7 %all-gather.10.cloned.1.call-start = ((), (), s32[]{:S(2)}) async-start(), calls=%async_computation.4 | async-start | bytes 2506752 | tf_op jit(solution)/shard_map/all_gather | solution.py:183
  12.2 253.1 %reduce-scatter.5.cloned.1.call-start = ((), (), s32[]{:S(2)}) async-start(), calls=%async_computation.6 | async-start | bytes 1179648 | tf_op jit(solution)/shard_map/reduce_scatter | solution.py:328
  38.1 166.5 %copy-start.10 = (bf16[641,384]{0,1:T(8,128)(2,1)}, bf16[641,384]{0,1:T(8,128)(2,1)S(1)}, u32[]{:S(2)}) copy-start(bf16[641,384]{0,1:T(8,128)(2,1)S(1)} %all_gather.27) | copy-start | bytes 1476868
  58.1 25.5 %copy-start.18 = (bf16[2,384,384]{2,1,0:T(8,128)(2,1)}, bf16[2,384,384]{2,1,0:T(8,128)(2,1)S(1)}, u32[]{:S(2)}) copy-start(bf16[2,384,384]{2,1,0:T(8,128)(2,1)S(1)} %all_gather.28) | copy-start | bytes 1769476
  246.7 38.3 %reduce-scatter.3.cloned.1.call-start = ((), (), s32[]{:S(2)}) async-start(), calls=%async_computation.5 | async-start | bytes 1179648 | tf_op jit(solution)/shard_map/reduce_scatter | solution.py:322
  249.9 323.6 %all-reduce.18.cloned.1.call-start = ((), (), s32[]{:S(2)}) async-start(), calls=%async_computation.9 | async-start | bytes 25952256 | tf_op jit(solution)/shard_map/psum | solution.py:351
  262.0 22.9 %copy-start.75 = (bf16[512,6,64]{0,2,1:T(8,128)(2,1)S(1)}, bf16[512,6,64]{0,2,1:T(8,128)(2,1)}, u32[]{:S(2)}) copy-start(bf16[512,6,64]{0,2,1:T(8,128)(2,1)} %convert.18) | copy-start | bytes 1179652
  262.1 22.9 %copy-start.78 = (bf16[384,384]{1,0:T(8,128)(2,1)S(1)}, bf16[384,384]{1,0:T(8,128)(2,1)}, u32[]{:S(2)}) copy-start(bf16[384,384]{1,0:T(8,128)(2,1)} %copy-done.77) | copy-start | bytes 884740
  336.6 280.4 %copy-start.86 = (f32[4,24,384]{2,1,0:T(8,128)S(1)}, f32[4,24,384]{2,1,0:T(8,128)}, u32[]{:S(2)}) copy-start(f32[4,24,384]{2,1,0:T(8,128)} %param.32) | copy-start | bytes 442372
  336.6 282.1 %copy-start.83 = (f32[2,24,1536]{2,1,0:T(8,128)S(1)}, f32[2,24,1536]{2,1,0:T(8,128)}, u32[]{:S(2)}) copy-start(f32[2,24,1536]{2,1,0:T(8,128)} %param.34) | copy-start | bytes 884740
  336.7 285.9 %copy-start.81 = (f32[2,24,384]{2,1,0:T(8,128)S(1)}, f32[2,24,384]{2,1,0:T(8,128)}, u32[]{:S(2)}) copy-start(f32[2,24,384]{2,1,0:T(8,128)} %param.38) | copy-start | bytes 221188
  336.7 285.9 %copy-start.87 = (f32[2,24,384]{2,1,0:T(8,128)S(1)}, f32[2,24,384]{2,1,0:T(8,128)}, u32[]{:S(2)}) copy-start(f32[2,24,384]{2,1,0:T(8,128)} %param.40) | copy-start | bytes 221188
  336.7 285.9 %copy-start.88 = (f32[2,24,384]{2,1,0:T(8,128)S(1)}, f32[2,24,384]{2,1,0:T(8,128)}, u32[]{:S(2)}) copy-start(f32[2,24,384]{2,1,0:T(8,128)} %param.39) | copy-start | bytes 221188
  336.7 287.5 %copy-start.82 = (f32[641,24]{0,1:T(8,128)S(1)}, f32[641,24]{0,1:T(8,128)}, u32[]{:S(2)}) copy-start(f32[641,24]{0,1:T(8,128)} %param.41) | copy-start | bytes 184612
  336.7 287.5 %copy-start.89 = (f32[641,24]{0,1:T(8,128)S(1)}, f32[641,24]{0,1:T(8,128)}, u32[]{:S(2)}) copy-start(f32[641,24]{0,1:T(8,128)} %param.43) | copy-start | bytes 184612
  336.7 287.4 %copy-start.90 = (f32[641,24]{0,1:T(8,128)S(1)}, f32[641,24]{0,1:T(8,128)}, u32[]{:S(2)}) copy-start(f32[641,24]{0,1:T(8,128)} %param.42) | copy-start | bytes 184612
  336.7 289.0 %copy-start.57 = (f32[24,2304]{1,0:T(8,128)S(1)}, f32[24,2304]{1,0:T(8,128)}, u32[]{:S(2)}) copy-start(f32[24,2304]{1,0:T(8,128)} %param.35) | copy-start | bytes 663556
  336.8 289.0 %copy-start.84 = (f32[24,2304]{1,0:T(8,128)S(1)}, f32[24,2304]{1,0:T(8,128)}, u32[]{:S(2)}) copy-start(f32[24,2304]{1,0:T(8,128)} %param.37) | copy-start | bytes 663556
  336.8 289.0 %copy-start.85 = (f32[24,2304]{1,0:T(8,128)S(1)}, f32[24,2304]{1,0:T(8,128)}, u32[]{:S(2)}) copy-start(f32[24,2304]{1,0:T(8,128)} %param.36) | copy-start | bytes 663556
  336.8 322.1 %all-gather.12.cloned.1.call-start = ((), (), s32[]{:S(2)}) async-start(), calls=%async_computation.7 | async-start | bytes 2506752 | tf_op jit(solution)/shard_map/all_gather | solution.py:376
  618.7 118.3 %all-gather.14.cloned.1.call-start = ((), (), s32[]{:S(2)}) async-start(), calls=%async_computation.8 | async-start | bytes 5013504 | tf_op jit(solution)/shard_map/all_gather | solution.py:377
  (114 other events, 495.5 us)
Sparse Core Ops, SparseCore 0:
  10.8 43.4 all-gather.7
  57.0 38.8 all-gather.5
  98.8 41.1 all-gather.9
  246.8 18.4 reduce-scatter.4
  267.4 17.4 reduce-scatter.2
  336.8 236.7 all-reduce.17
  618.8 40.0 all-gather.11
  661.7 51.6 all-gather.13
where the time goes:
time: 856 us; the launch traced here: 846 us
  waiting for transfers between devices  298 us (35%)
  matrix products  277 us (32%)
  blocking collectives  138 us (16%)
  other arithmetic  58.3 us (7%)
  local copies, waits for them, and re-layouts  49.3 us (6%)
  between operations  25.1 us (3%)
    psum x1, waiting for transfers between devices, body(): lax.psum((grads[0], grads[1], grads[2], grads[3], grads[4]), ('dp', 'seq'))  237 us
    dot_general x44, matrix products, high_dot(): return jnp.dot(a, b, precision=highest, preferred_element_type=jnp.float32)  196 us
    psum x1, blocking collectives, body(): loss_total = lax.psum(loss_part, ('dp', 'seq'))  38.5 us
    psum x1, blocking collectives, body(): square_total = lax.psum(square_part, 'dp')  31.7 us
    all_gather x1, waiting for transfers between devices, body(): lax.all_gather(attention_fresh, 'dp', axis=1, tiled=True)  31.2 us
    all_gather x1, blocking collectives, body(): lax.all_gather(lookup_table.astype(jnp.bfloat16), 'dp', axis=1, tiled=True)  24.9 us
    reduce_scatter x1, waiting for transfers between devices, body(): lax.psum_scatter(dkey_stack.reshape(length, D).astype(jnp.bfloat16), 'seq...  19.6 us
    all_gather x1, blocking collectives, body(): lax.all_gather(pooling_mats.astype(jnp.bfloat16), 'dp', axis=1, tiled=True)  19.4 us
  transfers between devices with their start and end apart: 8, of which 5 were waited for; matrix products, arithmetic and copies ran while one was open for 20% of the time, Pallas kernels for 0%

commit v1 on v0

--- a/solution.py
+++ b/solution.py
@@ -149,6 +149,37 @@
         first_hat / (jnp.sqrt(second_hat) + adam_eps) + adam_decay * weight
     )
     return (weight_new, first_new, second_new)
+
+
+def split_high(a):
+    upper = a.astype(jnp.bfloat16)
+    return upper, (a - upper.astype(jnp.float32)).astype(jnp.bfloat16)
+
+
+def mid_dot(a, b):
+    return jnp.dot(a, b, precision=lax.Precision.HIGH, preferred_element_type=jnp.float32)
+
+
+def orth_square(matrix):
+    current = matrix / (jnp.sqrt(jnp.sum(matrix * matrix)) + 1e-07)
+    for sweep in range(5):
+        gram = mid_dot(current, current.T)
+        polynomial = ns_b * gram + ns_c * mid_dot(gram, gram)
+        current = ns_a * current + mid_dot(polynomial, current)
+    return current
+
+
+def orth_wide(matrix):
+    start = matrix / (jnp.sqrt(jnp.sum(matrix * matrix)) + 1e-07)
+    gram = mid_dot(start, start.T)
+    eye = jnp.eye(matrix.shape[0], dtype=jnp.float32)
+    product = None
+    for sweep in range(5):
+        polynomial = ns_a * eye + ns_b * gram + ns_c * mid_dot(gram, gram)
+        product = polynomial if product is None else mid_dot(polynomial, product)
+        if sweep < 4:
+            gram = mid_dot(mid_dot(polynomial, gram), polynomial)
+    return mid_dot(product, start)
 
 
 def body(
@@ -178,76 +209,59 @@
     head_dim = D // HEADS
     scale = 1.0 / math.sqrt(head_dim)
     width_in, lead_at, query_at, bias_at, head_at = offsets()
-    gathered = (
-        lax.all_gather(attention_mats.astype(jnp.bfloat16), "dp", axis=1, tiled=True),
-        lax.all_gather(feedforward_mats.astype(jnp.bfloat16), "dp", axis=1, tiled=True),
-        lax.all_gather(modulation_mat.astype(jnp.bfloat16), "dp", axis=0, tiled=True),
-        lax.all_gather(pooling_mats.astype(jnp.bfloat16), "dp", axis=1, tiled=True),
-        lax.all_gather(lookup_table.astype(jnp.bfloat16), "dp", axis=1, tiled=True),
-    )
-    attention_b, feed_b, mod_b, pool_b, lookup_b = gathered
+    own = attention_mats.shape[1]
+    place = lax.axis_index("dp")
+    here = lax.axis_index("seq")
+    table_own = lookup_table.T.astype(jnp.bfloat16)
+    lookup_t = lax.all_gather(table_own, "dp", axis=0, tiled=True)
+    pool_b = lax.all_gather(pooling_mats.astype(jnp.bfloat16), "dp", axis=1, tiled=True)
+    attention_b = lax.all_gather(attention_mats.astype(jnp.bfloat16), "dp", axis=1, tiled=True)
+    feed_b = lax.all_gather(feedforward_mats.astype(jnp.bfloat16), "dp", axis=1, tiled=True)
     present = presence(counts[0])
-    first_row = lax.axis_index("seq") * rows
+    mod_own = modulation_mat.astype(jnp.bfloat16).astype(jnp.float32)
+    lead_own = table_own[:, lead_at:query_at].astype(jnp.float32)
+    cond_own, cond_back = jax.vjp(jax.nn.silu, lead_own)
+    lead_part = lax.dot_general(
+        cond_own, mod_own, (((0,), (0,)), ((), ())), precision=highest,
+        preferred_element_type=jnp.float32,
+    )
+    count_row = jnp.full((1, 6 * D), jnp.sum(present), jnp.float32)
+    lead_all = lax.psum(jnp.concatenate([lead_part, count_row]), "dp")
+    bias_rows = lookup_t[:, bias_at:head_at].T.astype(jnp.float32)
+    lead_hot = (jnp.arange(NLEAD, dtype=jnp.int32) == lead_step[0]).astype(jnp.float32)
+    modul = (
+        jnp.sum(lead_hot[:, None] * lead_all[:NLEAD], axis=0).reshape(6, D) + bias_rows
+    )
+    first_row = here * rows
     lat = lat_weight(first_row, rows, 2 * length // PCOLS)
+    lat_all = lat_weight(0, length, 2 * length // PCOLS)
     weight = (lat[:, None, :] * present[None, :, None]).reshape(rows, width_in)
-    weight_total = lax.psum(jnp.sum(weight), ("dp", "seq"))
+    weight_total = jnp.sum(lat_all) * lead_all[NLEAD, 0]
     pix_rows = fields[0].astype(jnp.float32)
 
-    def prelude(lookup_f, mod_f, pool_f):
-        return (
-            aggregate(lookup_f, pool_f[0], pool_f[1], pix_rows, present),
-            modulation(lookup_f, mod_f, lead_step[0]),
-        )
-
-    (stream_in, modul), prelude_back = jax.vjp(
-        prelude, lookup_b.astype(jnp.float32), mod_b.astype(jnp.float32), pool_b.astype(jnp.float32)
+    def prelude(lookup_f, pool_f):
+        return aggregate(lookup_f.T, pool_f[0], pool_f[1], pix_rows, present)
+
+    stream_in, prelude_back = jax.vjp(
+        prelude, lookup_t.astype(jnp.float32), pool_b.astype(jnp.float32)
     )
     entry, entry_back = jax.vjp(entry_fn, stream_in, modul)
     entry_b = entry.astype(jnp.bfloat16)
-    joined = jnp.concatenate([attention_b[0], attention_b[1], attention_b[2]], axis=1)
-    triple = plain_dot(entry_b, joined)
-    queries = triple[:, :D].astype(jnp.bfloat16).reshape(rows, HEADS, head_dim)
-    keys = triple[:, D : 2 * D].astype(jnp.bfloat16)
-    values = triple[:, 2 * D :].astype(jnp.bfloat16)
-    keys_all, values_all = (
-        lax.all_gather(keys, "seq", axis=0, tiled=True),
-        lax.all_gather(values, "seq", axis=0, tiled=True),
-    )
-    block = math.gcd(512, length)
-    pairs = (
-        keys_all.reshape(length // block, block, HEADS, head_dim),
-        values_all.reshape(length // block, block, HEADS, head_dim),
-    )
-
-    def block_scores(query_part, key_block):
-        return (
-            jnp.einsum("qhc,khc->hqk", query_part, key_block, preferred_element_type=jnp.float32)
-            * scale
-        )
-
-    def totals_step(carry, key_block):
-        running, total = carry
-        scores = block_scores(queries, key_block)
-        top = jnp.maximum(running, jnp.max(scores, axis=-1))
-        total = total * jnp.exp(running - top) + jnp.sum(jnp.exp(scores - top[:, :, None]), axis=-1)
-        return ((top, total), None)
-
-    start = (jnp.full((HEADS, rows), -jnp.inf, jnp.float32), jnp.zeros((HEADS, rows), jnp.float32))
-    (top, total), unused = lax.scan(totals_step, start, pairs[0])
-    log_total = top + jnp.log(total)
-
-    def probs_of(key_block):
-        return jnp.exp(block_scores(queries, key_block) - log_total[:, :, None])
-
-    def output_step(carry, pair):
-        probs_b = probs_of(pair[0]).astype(jnp.bfloat16)
-        return (
-            carry
-            + jnp.einsum("hqk,khc->qhc", probs_b, pair[1], preferred_element_type=jnp.float32),
-            None,
-        )
-
-    attended, unused = lax.scan(output_step, jnp.zeros((rows, HEADS, head_dim), jnp.float32), pairs)
+    entry_all = lax.all_gather(entry_b, "seq", axis=0, tiled=True)
+    queries = plain_dot(entry_b, attention_b[0]).astype(jnp.bfloat16)
+    keys = plain_dot(entry_all, attention_b[1]).astype(jnp.bfloat16)
+    values = plain_dot(entry_all, attention_b[2]).astype(jnp.bfloat16)
+    queries_h = queries.reshape(rows, HEADS, head_dim)
+    keys_h = keys.reshape(length, HEADS, head_dim)
+    values_h = values.reshape(length, HEADS, head_dim)
+    scores = (
+        jnp.einsum("qhc,khc->hqk", queries_h, keys_h, preferred_element_type=jnp.float32) * scale
+    )
+    top = jnp.max(scores, axis=-1, keepdims=True)
+    log_total = top + jnp.log(jnp.sum(jnp.exp(scores - top), axis=-1, keepdims=True))
+    probs = jnp.exp(scores - log_total)
+    probs_b = probs.astype(jnp.bfloat16)
+    attended = jnp.einsum("hqk,khc->qhc", probs_b, values_h, preferred_element_type=jnp.float32)
     attended_b = attended.reshape(rows, D).astype(jnp.bfloat16)
     branch = plain_dot(attended_b, attention_b[3])
     (stream_mid, inner), middle_back = jax.vjp(middle_fn, stream_in, modul, branch)
@@ -258,13 +272,13 @@
     lowered = contract_last(hidden_b, feed_b[1])
     final, closing_back = jax.vjp(closing_fn, stream_mid, modul, lowered)
     final_b = final.astype(jnp.bfloat16)
-    head_b = lookup_b[head_at:]
-    pred = contract_last(final_b, head_b)
+    head_t = lookup_t[:, head_at:]
+    pred = plain_dot(final_b, head_t)
     miss = pred - targets[0]
     loss_part = jnp.sum(weight * miss * miss)
     dpred_b = (2.0 * weight * miss / weight_total).astype(jnp.bfloat16)
-    dfinal = plain_dot(dpred_b, head_b)
-    dhead = contract_first(dpred_b, final_b)
+    dfinal = contract_last(dpred_b, head_t)
+    dhead_t = contract_first(final_b, dpred_b)
     dstream_c, dmodul_c, dlowered = closing_back(dfinal)
     dlowered_b = dlowered.astype(jnp.bfloat16)
     dhidden = plain_dot(dlowered_b, feed_b[1])
@@ -274,115 +288,83 @@
     dup = contract_first(inner_b, dupper_b)
     dstream_m, dmodul_m, dbranch = middle_back((dstream_c, dinner))
     dbranch_b = dbranch.astype(jnp.bfloat16)
-    dattended_b = (
-        contract_last(dbranch_b, attention_b[3]).astype(jnp.bfloat16).reshape(rows, HEADS, head_dim)
-    )
+    dattended_b = contract_last(dbranch_b, attention_b[3]).astype(jnp.bfloat16)
+    dattended_h = dattended_b.reshape(rows, HEADS, head_dim)
     dout_w = contract_first(attended_b, dbranch_b)
-
-    def block_dprobs(grad_part, value_block):
-        return jnp.einsum(
-            "qhc,khc->hqk", grad_part, value_block, preferred_element_type=jnp.float32
-        )
-
-    def delta_step(carry, pair):
-        return (
-            carry + jnp.sum(probs_of(pair[0]) * block_dprobs(dattended_b, pair[1]), axis=-1),
-            None,
-        )
-
-    delta, unused = lax.scan(delta_step, jnp.zeros((HEADS, rows), jnp.float32), pairs)
-
-    def grad_step(carry, pair):
-        key_block, value_block = pair
-        probs = probs_of(key_block)
-        dscores_b = (probs * (block_dprobs(dattended_b, value_block) - delta[:, :, None])).astype(
-            jnp.bfloat16
-        )
-        dqueries = (
-            carry
-            + jnp.einsum("hqk,khc->qhc", dscores_b, key_block, preferred_element_type=jnp.float32)
-            * scale
-        )
-        dkey_block = (
-            jnp.einsum("hqk,qhc->khc", dscores_b, queries, preferred_element_type=jnp.float32)
-            * scale
-        )
-        dvalue_block = jnp.einsum(
-            "hqk,qhc->khc",
-            probs.astype(jnp.bfloat16),
-            dattended_b,
-            preferred_element_type=jnp.float32,
-        )
-        return (dqueries, (dkey_block, dvalue_block))
-
-    dqueries, (dkey_stack, dvalue_stack) = lax.scan(
-        grad_step, jnp.zeros((rows, HEADS, head_dim), jnp.float32), pairs
-    )
-    dkeys_own, dvalues_own = (
-        lax.psum_scatter(
-            dkey_stack.reshape(length, D).astype(jnp.bfloat16),
-            "seq",
-            scatter_dimension=0,
-            tiled=True,
-        ).astype(jnp.float32),
-        lax.psum_scatter(
-            dvalue_stack.reshape(length, D).astype(jnp.bfloat16),
-            "seq",
-            scatter_dimension=0,
-            tiled=True,
-        ).astype(jnp.float32),
-    )
-    dtriple_b = jnp.concatenate([dqueries.reshape(rows, D), dkeys_own, dvalues_own], axis=1).astype(
-        jnp.bfloat16
-    )
-    dentry = contract_last(dtriple_b, joined)
-    djoined = contract_first(entry_b, dtriple_b)
+    dprobs = jnp.einsum("qhc,khc->hqk", dattended_h, values_h, preferred_element_type=jnp.float32)
+    delta = jnp.sum(probs * dprobs, axis=-1, keepdims=True)
+    dscores_b = (probs * (dprobs - delta)).astype(jnp.bfloat16)
+    dqueries = (
+        jnp.einsum("hqk,khc->qhc", dscores_b, keys_h, preferred_element_type=jnp.float32) * scale
+    )
+    dkeys = (
+        jnp.einsum("hqk,qhc->khc", dscores_b, queries_h, preferred_element_type=jnp.float32) * scale
+    )
+    dvalues = jnp.einsum("hqk,qhc->khc", probs_b, dattended_h, preferred_element_type=jnp.float32)
+    dqueries_b = dqueries.reshape(rows, D).astype(jnp.bfloat16)
+    dkeys_b = dkeys.reshape(length, D).astype(jnp.bfloat16)
+    dvalues_b = dvalues.reshape(length, D).astype(jnp.bfloat16)
+    dentry_all = contract_last(dkeys_b, attention_b[1]) + contract_last(dvalues_b, attention_b[2])
+    dentry_far = lax.psum_scatter(
+        dentry_all.astype(jnp.bfloat16), "seq", scatter_dimension=0, tiled=True
+    )
+    dentry = contract_last(dqueries_b, attention_b[0]) + dentry_far.astype(jnp.float32)
+    dquery_w = contract_first(entry_b, dqueries_b)
+    dkey_w = contract_first(entry_all, dkeys_b)
+    dvalue_w = contract_first(entry_all, dvalues_b)
     dstream_e, dmodul_e = entry_back(dentry)
-    dlookup, dmod, dpool = prelude_back((dstream_m + dstream_e, dmodul_c + dmodul_m + dmodul_e))
-    dlookup = dlookup + jnp.pad(dhead, ((head_at, 0), (0, 0)))
-    grads = (
-        jnp.stack([djoined[:, :D], djoined[:, D : 2 * D], djoined[:, 2 * D :], dout_w]),
-        jnp.stack([dup, ddown]),
-        dmod,
-        dpool,
-        dlookup,
-    )
-    dims = (1, 1, 0, 1, 1)
-    totals = lax.psum((grads[0], grads[1], grads[2], grads[3], grads[4]), ("dp", "seq"))
-    place = lax.axis_index("dp")
-    shares = tuple(
-        (
-            lax.dynamic_slice_in_dim(
-                whole,
-                place * (whole.shape[axis] // data_count),
-                whole.shape[axis] // data_count,
-                axis,
-            )
-            for whole, axis in zip(totals, dims)
-        )
-    )
+    dlookup_t, dpool = prelude_back(dstream_m + dstream_e)
+    dmodul = dmodul_c + dmodul_m + dmodul_e
+    dlead = lax.psum(lead_hot[:, None] * dmodul.reshape(1, 6 * D), ("dp", "seq"))
+    dlookup_t = dlookup_t + jnp.pad(dhead_t, ((0, 0), (head_at, 0)))
+    packed = jnp.concatenate(
+        [dup, ddown, dquery_w, dkey_w, dvalue_w, dout_w, dpool[0], dpool[1],
+         jnp.pad(dlookup_t, ((0, 0), (0, 2 * D - dlookup_t.shape[1])))],
+        axis=1,
+    ).astype(jnp.bfloat16)
+    share = lax.psum(
+        lax.psum_scatter(packed, "dp", scatter_dimension=0, tiled=True), "seq"
+    ).astype(jnp.float32)
+    wide = feedforward_mats.shape[2]
+    feed_share = jnp.stack([share[:, :wide], share[:, wide : 2 * wide]])
+    base = 2 * wide
+    attention_share = jnp.stack([share[:, base + D * k : base + D * (k + 1)] for k in range(4)])
+    pool_share = jnp.stack([share[:, base + D * k : base + D * (k + 1)] for k in (4, 5)])
+    table_share = share[:, base + 6 * D : base + 6 * D + lookup_table.shape[0]]
+    mod_share = high_dot(cond_own, dlead)
+    dcond = lax.dot_general(
+        mod_own, dlead, (((1,), (1,)), ((), ())), precision=highest,
+        preferred_element_type=jnp.float32,
+    )
+    dlead_own = cond_back(dcond)[0]
+    dbias = jnp.sum(dlead, axis=0).reshape(6, D).T
+    dbias_own = lax.dynamic_slice_in_dim(dbias, place * own, own, 0)
+    table_share = table_share + jnp.pad(
+        jnp.concatenate([dlead_own, jnp.zeros((own, HEADS), jnp.float32), dbias_own], axis=1),
+        ((0, 0), (lead_at, lookup_table.shape[0] - head_at)),
+    )
+    shares = (attention_share, feed_share, mod_share, pool_share, table_share)
     square_part = jnp.float32(0.0)
-    for share in shares:
-        square_part = square_part + jnp.sum(share * share)
-    loss_total = lax.psum(loss_part, ("dp", "seq"))
-    square_total = lax.psum(square_part, "dp")
-    loss = loss_total / weight_total
-    grad_norm = jnp.sqrt(square_total)
+    for part in shares:
+        square_part = square_part + jnp.sum(part * part)
+    sums = lax.psum(jnp.stack([square_part / seq_count, loss_part]), ("dp", "seq"))
+    loss = sums[1] / weight_total
+    grad_norm = jnp.sqrt(sums[0])
     factor = clip_limit / jnp.maximum(grad_norm, clip_limit)
-    clipped = [share * factor for share in shares]
+    clipped = [part * factor for part in shares]
+    clipped[4] = clipped[4].T
     attention_fresh = muon_mu * attention_mom + clipped[0]
     feedforward_fresh = muon_mu * feedforward_mom + clipped[1]
     whole_attention, whole_feed = (
-        lax.all_gather(attention_fresh, "dp", axis=1, tiled=True),
-        lax.all_gather(feedforward_fresh, "dp", axis=1, tiled=True),
-    )
-    rows_own = attention_mom.shape[1]
-    row_start = lax.axis_index("dp") * rows_own
+        lax.all_gather(attention_fresh.astype(jnp.bfloat16), "dp", axis=1, tiled=True),
+        lax.all_gather(feedforward_fresh.astype(jnp.bfloat16), "dp", axis=1, tiled=True),
+    )
+    row_start = place * own
     attention_orth = lax.dynamic_slice_in_dim(
-        jax.vmap(orthogonalize)(whole_attention), row_start, rows_own, 1
+        jax.vmap(orth_square)(whole_attention.astype(jnp.float32)), row_start, own, 1
     )
     feed_orth = lax.dynamic_slice_in_dim(
-        jax.vmap(orthogonalize)(whole_feed), row_start, rows_own, 1
+        jax.vmap(orth_wide)(whole_feed.astype(jnp.float32)), row_start, own, 1
     )
     attention_new = attention_mats * (1.0 - muon_rate * muon_decay) - muon_rate * attention_orth
     feedforward_new = feedforward_mats * (1.0 - muon_rate * muon_decay) - muon_rate * feed_orth

time: 856 us -> 697 us (0.81)
  matrix products: 277 us -> 166 us
  blocking collectives: 138 us -> 95 us
  waiting for transfers between devices: 298 us -> 333 us
  local copies, waits for them, and re-layouts: 49.3 us -> 25.2 us
  other arithmetic: 58.3 us -> 42.3 us
    dot_general x44 -> x14, matrix products: 196 us -> 19.1 us  [high_dot(): return jnp.dot(a, b, precision=highest, preferred_element_type=jnp.float32)]
    psum x1 -> x3, waiting for transfers between devices: 237 us -> 162 us  [the longest x1 119 us: body(): lax.psum(lead_hot[:, None] * dmodul.reshape(1, 6 * D), ('dp', 'seq'))]
    dot_general x18 -> x42, matrix products: 25.6 us -> 97.5 us  [the longest x34 72.4 us: mid_dot(): jnp.dot(a, b, precision=lax.Precision.HIGH, preferred_element_type=jnp.fl...]
    reduce_scatter x2, waiting for transfers between devices: 20.4 us -> 80.2 us  [the longest x1 79.1 us: body(): lax.psum_scatter(packed, 'dp', scatter_dimension=0, tiled=True)]
    psum x2 -> x1, blocking collectives: 70.2 us -> 39.3 us  [body(): lax.psum(jnp.stack([square_part / seq_count, loss_part]), ('dp', 'seq'))]
    all_gather x1, waiting for transfers between devices: 0.01 us -> 30 us  [body(): lax.all_gather(feedforward_mats.astype(jnp.bfloat16), 'dp', axis=1, tiled...]
    all_gather x1, waiting for transfers between devices: 0.02 us -> 26.7 us  [body(): lax.all_gather(attention_mats.astype(jnp.bfloat16), 'dp', axis=1, tiled=T...]
    all_gather x3 -> x2, blocking collectives: 48 us -> 36.6 us  [the longest x1 25 us: body(): lookup_t = lax.all_gather(table_own, 'dp', axis=0, tiled=True)]
  transfers between devices with their start and end apart: 8 -> 9, of which waited for: 5 -> 9; matrix products, arithmetic and copies ran while one was open for 20% -> 16% of each run, Pallas kernels for 0% -> 0%
where the time goes in v1:
time: 697 us; the launch traced here: 688 us
  waiting for transfers between devices  333 us (48%)
  matrix products  166 us (24%)
  blocking collectives  95 us (14%)
  other arithmetic  42.3 us (6%)
  between operations  25.9 us (4%)
  local copies, waits for them, and re-layouts  25.2 us (4%)
    psum x1, waiting for transfers between devices, body(): lax.psum(lead_hot[:, None] * dmodul.reshape(1, 6 * D), ('dp', 'seq'))  119 us
    reduce_scatter x1, waiting for transfers between devices, body(): lax.psum_scatter(packed, 'dp', scatter_dimension=0, tiled=True)  79.1 us
    dot_general x34, matrix products, mid_dot(): jnp.dot(a, b, precision=lax.Precision.HIGH, preferred_element_type=jnp.fl...  72.4 us
    psum x1, blocking collectives, body(): lax.psum(jnp.stack([square_part / seq_count, loss_part]), ('dp', 'seq'))  39.3 us
    all_gather x1, waiting for transfers between devices, body(): lax.all_gather(attention_fresh.astype(jnp.bfloat16), 'dp', axis=1, tiled=...  33.5 us
    all_gather x1, waiting for transfers between devices, body(): lax.all_gather(feedforward_mats.astype(jnp.bfloat16), 'dp', axis=1, tiled...  30 us
    all_gather x1, waiting for transfers between devices, body(): lax.all_gather(attention_mats.astype(jnp.bfloat16), 'dp', axis=1, tiled=T...  26.7 us
    all_gather x1, blocking collectives, body(): lookup_t = lax.all_gather(table_own, 'dp', axis=0, tiled=True)  25 us
  transfers between devices with their start and end apart: 9, of which 9 were waited for; matrix products, arithmetic and copies ran while one was open for 16% of the time, Pallas kernels for 0%

profile of v1, /device:TPU:0, one launch (start us, length us, event | category | flops | bytes accessed | tf_op | source)
XLA Modules:
  0.0 688.2 jit_solution(6624914987881688822)
XLA Ops:
  15.7 25.0 %all_gather.21 = bf16[384,641]{1,0:T(8,128)(2,1)S(1)} all-gather(bf16[24,641]{1,0:T(8,128)(2,1)S(1)} %convert_bitcast_fusion), channel_id=1, replica_groups=mesh['dp'=16,'seq'=2] {'dp'}, dimensions={0}, use_global_device_ids=true | all-gather | bytes 523056 | tf_op jit(solution)/shard_map/all_gather | solution.py:216
  41.4 19.2 %all_gather.22 = bf16[2,384,384]{2,1,0:T(8,128)(2,1)S(1)} all-gather(bf16[2,24,384]{2,1,0:T(8,128)(2,1)S(1)} %convert_element_type.190), channel_id=1, replica_groups=mesh['dp'=16,'seq'=2] {'dp'}, dimensions={1}, use_global_device_ids=true | all-gather | bytes 626688 | tf_op jit(solution)/shard_map/all_gather | solution.py:217
  64.3 3.1 convolution_bitcast_fusion.1
  69.2 3.6 fusion.126
  80.1 2.9 fusion.63
  84.8 19.5 %all-reduce.20.cloned.1.call-done = f32[9,2304]{1,0:T(8,128)} async-done(((f32[9,2304]{1,0:T(8,128)}), f32[9,2304]{1,0:T(8,128)}) %all-reduce.20.cloned.1.call-update) | async-done | bytes 82960 | tf_op jit(solution)/shard_map/psum | solution.py:229
  108.1 11.6 %all_gather.23 = bf16[1024,384]{0,1:T(8,128)(2,1)S(1)} all-gather(bf16[512,384]{0,1:T(8,128)(2,1)S(1)} %add_convert_fusion.3), channel_id=1, replica_groups=mesh['dp'=16,'seq'=2] {'seq'}, dimensions={0}, use_global_device_ids=true | all-gather | bytes 1179648 | tf_op jit(solution)/shard_map/all_gather | solution.py:250
  119.7 26.7 %all-gather.5.cloned.1.call-done = bf16[4,384,384]{2,1,0:T(8,128)(2,1)} async-done(((bf16[4,24,384]{2,1,0:T(8,128)(2,1)}), bf16[4,384,384]{2,1,0:T(8,128)(2,1)}) %all-gather.5.cloned.1.call-update) | async-done | bytes 1179664 | tf_op jit(solution)/shard_map/all_gather | solution.py:218
  160.5 30.0 %all-gather.7.cloned.1.call-done = bf16[2,384,1536]{2,1,0:T(8,128)(2,1)} async-done(((bf16[2,24,1536]{2,1,0:T(8,128)(2,1)}), bf16[2,384,1536]{2,1,0:T(8,128)(2,1)}) %all-gather.7.cloned.1.call-update) | async-done | bytes 2359312 | tf_op jit(solution)/shard_map/all_gather | solution.py:219
  198.0 2.9 fusion.15
  213.3 11.4 %multiply_reduce_fusion = (f32[6,512]{1,0:T(8,128)S(1)}, f32[6,512,1024]{2,1,0:T(8,128)}) fusion(f32[6,512,1024]{2,1,0:T(8,128)} %copy-done, f32[6,512]{1,0:T(8,128)S(1)} %copy-done.55, bf16[512,6,64]{0,2,1:T(8,128)(2,1)S(1)} %bitcast.298, bf16[1024,6,64]{0,2,1:T(8,128)(2,1)S(1)} %bitcast.285), kind=kOutput, calls=%fused_computation.1 | convolution fusion | flops 415233024 | bytes 26370048 | tf_op jit(solution)/shard_map/qhc,khc->hqk/dot_general | solution.py:294
  224.8 6.5 multiply_convert_fusion
  244.4 5.0 fusion.19
  261.2 3.3 fusion.5
  270.3 3.0 fusion.220
  284.8 119.3 %all-reduce.24.cloned.1.call-done = f32[8,2304]{1,0:T(8,128)} async-done(((f32[8,2304]{1,0:T(8,128)}), f32[8,2304]{1,0:T(8,128)}) %all-reduce.24.cloned.1.call-update) | async-done | bytes 73744 | tf_op jit(solution)/shard_map/psum | solution.py:318
  406.3 79.1 %reduce-scatter.7.cloned.1.call-done = bf16[24,6144]{1,0:T(8,128)(2,1)} async-done(((bf16[384,6144]{1,0:T(8,128)(2,1)}), bf16[24,6144]{1,0:T(8,128)(2,1)}) %reduce-scatter.7.cloned.1.call-update) | async-done | bytes 294928 | tf_op jit(solution)/shard_map/reduce_scatter | solution.py:326
  487.5 23.2 %all-reduce.22.cloned.1.call-done = bf16[24,6144]{1,0:T(8,128)(2,1)} async-done(((bf16[24,6144]{1,0:T(8,128)(2,1)}), bf16[24,6144]{1,0:T(8,128)(2,1)}) %all-reduce.22.cloned.1.call-update) | async-done | bytes 294928 | tf_op jit(solution)/shard_map/psum | solution.py:325
  518.4 39.3 %psum.31 = f32[2]{0:T(128)S(1)} all-reduce(f32[2]{0:T(128)S(1)} %pad_maximum_fusion.4), channel_id=1, replica_groups=mesh['dp'=16,'seq'=2] {'dp','seq'}, use_global_device_ids=true, to_apply=%region_41.42 | all-reduce | flops 2 | bytes 16 | tf_op jit(solution)/shard_map/psum | solution.py:350
  566.1 33.5 %all-gather.9.cloned.1.call-done = bf16[4,384,384]{2,0,1:T(4,128)(2,1)} async-done(((bf16[4,24,384]{2,0,1:T(4,128)(2,1)}), bf16[4,384,384]{2,0,1:T(4,128)(2,1)}) %all-gather.9.cloned.1.call-update) | async-done | bytes 1179664 | tf_op jit(solution)/shard_map/all_gather | solution.py:359
  601.3 4.1 fusion.56
  626.1 3.0 fusion.226
  646.2 4.0 fusion.17
  674.1 4.1 fusion.16
  (445 shorter events, 179.0 us)
Async XLA Ops:
  7.2 97.1 %all-reduce.20.cloned.1.call-start = ((), (), s32[]{:S(2)}) async-start(), calls=%async_computation.2 | async-start | bytes 294912 | tf_op jit(solution)/shard_map/psum | solution.py:229
  8.1 53.2 %copy-start.64 = (bf16[24,641]{1,0:T(8,128)(2,1)}, bf16[24,641]{1,0:T(8,128)(2,1)S(1)}, u32[]{:S(2)}) copy-start(bf16[24,641]{1,0:T(8,128)(2,1)S(1)} %convert_bitcast_fusion) | copy-start | bytes 92308
  12.2 134.2 %all-gather.5.cloned.1.call-start = ((), (), s32[]{:S(2)}) async-start(), calls=%async_computation.3 | async-start | bytes 1253376 | tf_op jit(solution)/shard_map/all_gather | solution.py:218
  13.9 176.6 %all-gather.7.cloned.1.call-start = ((), (), s32[]{:S(2)}) async-start(), calls=%async_computation.4 | async-start | bytes 2506752 | tf_op jit(solution)/shard_map/all_gather | solution.py:219
  15.6 241.2 %reduce-scatter.5.cloned.1.call-start = ((), (), s32[]{:S(2)}) async-start(), calls=%async_computation.5 | async-start | bytes 1179648 | tf_op jit(solution)/shard_map/reduce_scatter | solution.py:308
  15.7 62.4 %copy-start.97 = (pred[69]{0:T(512)(128)(4,1)}, pred[69]{0:T(512)(128)(4,1)S(1)}, u32[]{:S(2)}) copy-start(pred[69]{0:T(512)(128)(4,1)S(1)} %get-tuple-element.142) | copy-start | bytes 211
  41.0 64.3 %copy-start.30 = (bf16[384,641]{0,1:T(8,128)(2,1)}, bf16[384,641]{0,1:T(8,128)(2,1)S(1)}, u32[]{:S(2)}) copy-start(bf16[384,641]{0,1:T(8,128)(2,1)S(1)} %copy.328) | copy-start | bytes 1476868
  84.6 64.9 %copy-start.86 = (f32[512]{0:T(512)}, f32[512]{0:T(512)S(1)}, u32[]{:S(2)}) copy-start(f32[512]{0:T(512)S(1)} %broadcast_multiply_fusion.4) | copy-start | bytes 6148
  84.8 64.8 %copy-start.93 = (f32[512]{0:T(512)}, f32[512]{0:T(512)S(1)}, u32[]{:S(2)}) copy-start(f32[512]{0:T(512)S(1)} %fusion.176) | copy-start | bytes 6148
  105.4 53.6 %copy-start.83 = (f32[384]{0:T(512)}, f32[384]{0:T(512)S(1)}, u32[]{:S(2)}) copy-start(f32[384]{0:T(512)S(1)} %get-tuple-element.100) | copy-start | bytes 4612
  105.4 85.1 %copy-start.73 = (f32[384]{0:T(512)}, f32[384]{0:T(512)S(1)}, u32[]{:S(2)}) copy-start(f32[384]{0:T(512)S(1)} %get-tuple-element.97) | copy-start | bytes 4612
  105.4 85.1 %copy-start.99 = (f32[384]{0:T(512)}, f32[384]{0:T(512)S(1)}, u32[]{:S(2)}) copy-start(f32[384]{0:T(512)S(1)} %get-tuple-element.96) | copy-start | bytes 4612
  105.4 87.7 %copy-start.112 = (f32[384]{0:T(512)}, f32[384]{0:T(512)S(1)}, u32[]{:S(2)}) copy-start(f32[384]{0:T(512)S(1)} %get-tuple-element.95) | copy-start | bytes 4612
  240.3 163.7 %all-reduce.24.cloned.1.call-start = ((), (), s32[]{:S(2)}) async-start(), calls=%async_computation.7 | async-start | bytes 147456 | tf_op jit(solution)/shard_map/psum | solution.py:318
  283.6 201.8 %reduce-scatter.7.cloned.1.call-start = ((), (), s32[]{:S(2)}) async-start(), calls=%async_computation.10 | async-start | bytes 5013504 | tf_op jit(solution)/shard_map/reduce_scatter | solution.py:326
  284.6 120.6 %copy-start.40 = (f32[24,2304]{1,0:T(8,128)S(1)}, f32[24,2304]{1,0:T(8,128)}, u32[]{:S(2)}) copy-start(f32[24,2304]{1,0:T(8,128)} %param.27) | copy-start | bytes 663556
  284.6 274.4 %copy-start.67 = (f32[4,24,384]{2,1,0:T(8,128)S(1)}, f32[4,24,384]{2,1,0:T(8,128)}, u32[]{:S(2)}) copy-start(f32[4,24,384]{2,1,0:T(8,128)} %param.24) | copy-start | bytes 442372
  284.6 226.1 %all-reduce.22.cloned.1.call-start = ((), (), s32[]{:S(2)}) async-start(), calls=%async_computation.6 | async-start | bytes 589824 | tf_op jit(solution)/shard_map/psum | solution.py:325
  405.2 156.9 %copy-start.61 = (f32[2,24,1536]{2,1,0:T(8,128)S(1)}, f32[2,24,1536]{2,1,0:T(8,128)}, u32[]{:S(2)}) copy-start(f32[2,24,1536]{2,1,0:T(8,128)} %param.26) | copy-start | bytes 884740
  485.5 114.1 %all-gather.9.cloned.1.call-start = ((), (), s32[]{:S(2)}) async-start(), calls=%async_computation.8 | async-start | bytes 1253376 | tf_op jit(solution)/shard_map/all_gather | solution.py:359
  511.8 52.6 %copy-start.60 = (f32[641,24]{0,1:T(8,128)S(1)}, f32[641,24]{0,1:T(8,128)}, u32[]{:S(2)}) copy-start(f32[641,24]{0,1:T(8,128)} %param.33) | copy-start | bytes 184612
  511.8 53.3 %copy-start.65 = (f32[24,2304]{1,0:T(8,128)S(1)}, f32[24,2304]{1,0:T(8,128)}, u32[]{:S(2)}) copy-start(f32[24,2304]{1,0:T(8,128)} %param.29) | copy-start | bytes 663556
  511.8 53.3 %copy-start.66 = (f32[24,2304]{1,0:T(8,128)S(1)}, f32[24,2304]{1,0:T(8,128)}, u32[]{:S(2)}) copy-start(f32[24,2304]{1,0:T(8,128)} %param.28) | copy-start | bytes 663556
  560.4 83.3 %all-gather.11.cloned.1.call-start = ((), (), s32[]{:S(2)}) async-start(), calls=%async_computation.9 | async-start | bytes 2506752 | tf_op jit(solution)/shard_map/all_gather | solution.py:360
  (103 other events, 956.1 us)
Sparse Core Ops, SparseCore 0:
  12.4 91.8 all-reduce.19
  107.1 39.2 all-gather.4
  149.3 41.1 all-gather.6
  240.5 16.2 reduce-scatter.4
  283.8 120.2 all-reduce.23
  407.8 77.6 reduce-scatter.6
  487.7 22.9 all-reduce.21
  560.5 39.0 all-gather.8
  602.4 41.1 all-gather.10
